TPU v7x, 512 devices: a whole 4x4x16 slice. The times are simulated.
512 devices in a mesh: shift: 8 (over x, core), batch: 16 (over z), cols: 4 (over y).
Axes of the slice: x: 4, y: 4, z: 16, core: 2. Of those that a mesh axis runs over, the one named last changes fastest.
Arguments:
- partial_up: float32 [128, 768, 3072], P(('shift', 'batch'), None, 'cols'), parts along dimension 0, may hold values from -0.875 to 0.875
- partial_down: float32 [128, 3072, 768], P(('shift', 'batch'), 'cols'), parts along dimension 0, may hold values from -0.875 to 0.875
- partial_norm: float32 [128, 768], P(('shift', 'batch')), parts along dimension 0, may hold values from -8 to 8
- partial_bias: float32 [128, 768], P(('shift', 'batch')), parts along dimension 0, may hold values from -8 to 8
- master_up: float32 [6144, 3072], P(('shift', 'batch'), 'cols'), parts along dimension 0, may hold values from -0.21875 to 0.21875
- master_down: float32 [24576, 768], P(('shift', 'cols'), 'batch'), parts along dimension 0, may hold values from -0.109375 to 0.109375
- master_norm: float32 [6144], P(('shift', 'batch')), parts along dimension 0, may hold values from 0.25 to 1.75
- master_bias: float32 [6144], P(('shift', 'batch')), parts along dimension 0, may hold values from -3 to 3
- memory_up: float32 [6144, 3072], P(('shift', 'batch'), 'cols'), parts along dimension 0, may hold values from -1.75 to 1.75
- memory_down: float32 [24576, 768], P(('shift', 'cols'), 'batch'), parts along dimension 0, may hold values from -1.75 to 1.75
- memory_norm: float32 [6144], P(('shift', 'batch')), parts along dimension 0, may hold values from -1.75 to 1.75
- memory_bias: float32 [6144], P(('shift', 'batch')), parts along dimension 0, may hold values from -1.75 to 1.75
Outputs:
- compute_up: bfloat16 [6144, 3072], P('shift', 'cols'), parts along dimension 0
- compute_down: bfloat16 [24576, 768], P(('shift', 'cols')), parts along dimension 0
- compute_norm: bfloat16 [6144], P('shift'), parts along dimension 0
- compute_bias: bfloat16 [6144], P('shift'), parts along dimension 0
- stepped_up: float32 [6144, 3072], P(('shift', 'batch'), 'cols'), parts along dimension 0
- stepped_down: float32 [24576, 768], P(('shift', 'cols'), 'batch'), parts along dimension 0
- stepped_norm: float32 [6144], P(('shift', 'batch')), parts along dimension 0
- stepped_bias: float32 [6144], P(('shift', 'batch')), parts along dimension 0
- state_new_up: float32 [6144, 3072], P(('shift', 'batch'), 'cols'), parts along dimension 0
- state_new_down: float32 [24576, 768], P(('shift', 'cols'), 'batch'), parts along dimension 0
- state_new_norm: float32 [6144], P(('shift', 'batch')), parts along dimension 0
- state_new_bias: float32 [6144], P(('shift', 'batch')), parts along dimension 0
There are 8 independent parts, one for each index of `shift`. A program takes and returns all parts, laid end to end along the dimension named above; each array names one. Nothing has to cross between parts.
All inputs are finite; a program needn't handle non-finite values.
Results may differ from a plain program's by a relative error of at most 0.0085.
Values may be sent and summed in bfloat16 or wider, within the bound.
No kernel may reach another device: no remote copies, remote signals or barrier semaphores. Data moves between devices by JAX's collectives and lax.ppermute only.
A program may use at most 64 MiB of HBM per device.

v0:
```python
import jax
import jax.numpy as jnp
from jax import lax
from jax.sharding import PartitionSpec as P

learn_rate = 0.1
hold_rate = 0.8


def in_blocks(array, dim, devices):
    shape = array.shape
    tiles = array.reshape(*shape[:dim], devices, shape[dim] // devices, *shape[dim + 1 :])
    return jnp.moveaxis(tiles, dim, 0)


def one_scatter(arrays, axis, dims):
    devices = lax.axis_size(axis)
    tiles = [in_blocks(a, dim, devices) for a, dim in zip(arrays, dims)]
    lines = jnp.concatenate([b.reshape(devices, -1) for b in tiles], axis=1)
    span = max(16, -(-lines.shape[1] // 1024) * 8)
    lines = jnp.pad(lines, ((0, 0), (0, span * 128 - lines.shape[1]))).reshape(-1, 128)
    line, at, finished = (lax.psum_scatter(lines, axis, tiled=True).reshape(-1), 0, [])
    for b in tiles:
        part = b[0]
        finished.append(line[at : at + part.size].reshape(part.shape))
        at += part.size
    return tuple(finished)


def sent_to_all(array, axis):
    copies = jnp.broadcast_to(array, (lax.axis_size(axis), *array.shape))
    return lax.all_to_all(copies, axis, split_axis=0, concat_axis=0, tiled=True)


def of_everyone(array, axis):
    return sent_to_all(array, axis).sum(axis=0)


def in_one(arrays, axis):
    line, at, finished = (jnp.concatenate([a.reshape(-1) for a in arrays]), 0, [])
    so_far = of_everyone(line, axis)
    for a in arrays:
        finished.append(so_far[at : at + a.size].reshape(a.shape))
        at += a.size
    return tuple(finished)


def gather_turned(arrays, axis, dims):
    turned = [jnp.moveaxis(a, dim, 0) for a, dim in zip(arrays, dims)]
    both = jnp.concatenate([t.reshape(len(t), -1) for t in turned], axis=1)
    filled, at, finished = (lax.all_gather(both, axis, axis=0, tiled=True), 0, [])
    for t, dim in zip(turned, dims):
        slab = filled[:, at : at + t[0].size].reshape(-1, *t.shape[1:])
        finished.append(jnp.moveaxis(slab, 0, dim))
        at += t[0].size
    return tuple(finished)


def on_device(
    partial_up,
    partial_down,
    partial_norm,
    partial_bias,
    master_up,
    master_down,
    master_norm,
    master_bias,
    memory_up,
    memory_down,
    memory_norm,
    memory_bias,
):
    mean_up, mean_down = tuple(
        (
            part.astype(jnp.float32)
            for part in one_scatter(
                (partial_up[0].astype(jnp.bfloat16), partial_down[0].astype(jnp.bfloat16)),
                "batch",
                (0, 1),
            )
        )
    )
    whole_norm, whole_bias = in_one((partial_norm[0], partial_bias[0]), "batch")
    place = lax.axis_index("batch")
    mean_norm = lax.dynamic_slice_in_dim(
        whole_norm, place * master_norm.shape[0], master_norm.shape[0]
    )
    mean_bias = lax.dynamic_slice_in_dim(
        whole_bias, place * master_bias.shape[0], master_bias.shape[0]
    )
    mean_rate = lax.axis_size("batch") ** (-0.5)
    mean_up = mean_up * mean_rate
    mean_down = mean_down * mean_rate
    mean_norm = mean_norm * mean_rate
    mean_bias = mean_bias * mean_rate
    state_new_up = hold_rate * memory_up + mean_up
    stepped_up = master_up - learn_rate * state_new_up
    state_new_down = hold_rate * memory_down + mean_down
    stepped_down = master_down - learn_rate * state_new_down
    state_new_norm = hold_rate * memory_norm + mean_norm
    stepped_norm = master_norm - learn_rate * state_new_norm
    state_new_bias = hold_rate * memory_bias + mean_bias
    stepped_bias = master_bias - learn_rate * state_new_bias
    compute_up, compute_down, compute_norm, compute_bias = gather_turned(
        (
            stepped_up.astype(jnp.bfloat16),
            stepped_down.astype(jnp.bfloat16),
            stepped_norm.astype(jnp.bfloat16),
            stepped_bias.astype(jnp.bfloat16),
        ),
        "batch",
        (0, 1, 0, 0),
    )
    return (
        compute_up,
        compute_down,
        compute_norm,
        compute_bias,
        stepped_up,
        stepped_down,
        stepped_norm,
        stepped_bias,
        state_new_up,
        state_new_down,
        state_new_norm,
        state_new_bias,
    )


def solution(mesh):
    return jax.shard_map(
        on_device,
        mesh=mesh,
        in_specs=(
            P(("shift", "batch"), None, "cols"),
            P(("shift", "batch"), "cols", None),
            P(("shift", "batch"), None),
            P(("shift", "batch"), None),
            P(("shift", "batch"), "cols"),
            P(("shift", "cols"), "batch"),
            P(("shift", "batch")),
            P(("shift", "batch")),
            P(("shift", "batch"), "cols"),
            P(("shift", "cols"), "batch"),
            P(("shift", "batch")),
            P(("shift", "batch")),
        ),
        out_specs=(
            P("shift", "cols"),
            P(("shift", "cols"), None),
            P("shift"),
            P("shift"),
            P(("shift", "batch"), "cols"),
            P(("shift", "cols"), "batch"),
            P(("shift", "batch")),
            P(("shift", "batch")),
            P(("shift", "batch"), "cols"),
            P(("shift", "cols"), "batch"),
            P(("shift", "batch")),
            P(("shift", "batch")),
        ),
        check_vma=False,
    )
```

profile of v0, /device:TPU:6, one launch (start us, length us, event | category | flops | bytes accessed | tf_op | source)
XLA Modules:
  0.0 193.7 jit_solution(17056441579653898916)
XLA Ops:
  7.2 0.0 copy-start
  7.2 0.0 reduce-scatter.2.cloned.1.call-start
  7.2 1.9 convert_element_type.34
  9.2 1.4 convert_element_type.35
  10.6 0.0 copy-done
  10.6 1.5 copy.50
  12.0 3.0 %copy.51 = bf16[16,768,48]{2,1,0:T(8,128)(2,1)S(1)} copy(bf16[16,768,48]{1,2,0:T(8,128)(2,1)} %bitcast.11) | data formatting | bytes 2359296 | tf_op jit(solution)/shard_map/transpose | solution.py:13
  15.0 7.1 %reshape.64 = bf16[16,36864]{1,0:T(8,128)(2,1)} reshape(bf16[16,768,48]{2,1,0:T(8,128)(2,1)S(1)} %copy.51) | data formatting | bytes 2359296 | tf_op jit(solution)/shard_map/reshape | solution.py:19
  22.2 1.8 pad_maximum_fusion
  23.9 2.1 %reshape.65 = bf16[9216,128]{1,0:T(8,128)(2,1)} reshape(bf16[16,73728]{1,0:T(8,128)(2,1)S(1)} %pad_maximum_fusion) | data formatting | bytes 4718592 | tf_op jit(solution)/shard_map/reshape | solution.py:21
  26.1 0.0 copy-start.5
  26.1 0.0 copy-start.9
  26.1 0.0 copy-start.10
  26.1 0.0 copy-start.1
  26.1 0.0 copy-start.2
  26.1 0.0 copy-start.3
  26.2 0.0 copy-start.4
  26.2 0.0 reduce-scatter.2.cloned.1.call-update
  26.2 0.6 copy-done.5
  26.8 0.0 copy-done.6
  26.8 0.7 broadcast_in_dim.3
  27.5 15.2 %all-to-all-start = ((f32[16,1,1536]{2,1,0:T(1,128)}), f32[16,1,1536]{2,1,0:T(1,128)S(1)}, u32[]{:S(2)}, u32[]{:S(2)}) async-start(f32[16,1,1536]{2,1,0:T(1,128)} %broadcast_in_dim.3), calls=%async_computation.1 | async-start | bytes 196608 | tf_op jit(solution)/shard_map/all_to_all | solution.py:32
  42.7 0.0 all-gather.2.cloned.1.call-start
  42.8 13.6 %all-to-all-done = f32[16,1,1536]{2,1,0:T(1,128)S(1)} async-done(((f32[16,1,1536]{2,1,0:T(1,128)}), f32[16,1,1536]{2,1,0:T(1,128)S(1)}, u32[]{:S(2)}, u32[]{:S(2)}) %all-to-all-start) | async-done | bytes 98336 | tf_op jit(solution)/shard_map/all_to_all | solution.py:32
  56.4 0.1 reduce_sum.9
  56.5 0.0 copy-done.7
  56.5 0.0 copy-done.8
  56.5 0.0 copy-done.9
  56.5 0.0 copy-done.10
  56.5 0.6 convert_bitcast_fusion.1
  57.1 0.1 copy.55
  57.2 0.1 copy.54
  57.3 48.7 %reduce-scatter.2.cloned.1.call-done = bf16[576,128]{1,0:T(8,128)(2,1)} async-done(((bf16[9216,128]{1,0:T(8,128)(2,1)}), bf16[576,128]{1,0:T(8,128)(2,1)}) %reduce-scatter.2.cloned.1.call-update) | async-done | bytes 147472 | tf_op jit(solution)/shard_map/reduce_scatter | solution.py:22
  106.1 0.9 convert_multiply_fusion
  107.0 0.2 mul.72
  107.2 0.1 copy.52
  107.4 0.0 copy-done.1
  107.4 0.0 copy-done.2
  107.4 0.7 fusion
  108.1 0.0 copy-done.3
  108.1 0.0 copy-done.4
  108.1 0.7 convert_bitcast_fusion
  108.9 0.8 concatenate.11
  109.6 0.0 all-gather.2.cloned.1.call-update
  109.6 71.1 %all-gather.2.cloned.1.call-done = bf16[768,1538]{1,0:T(8,128)(2,1)} async-done(((bf16[48,1538]{1,0:T(8,128)(2,1)}), bf16[768,1538]{1,0:T(8,128)(2,1)}) %all-gather.2.cloned.1.call-update) | async-done | bytes 2362384 | tf_op jit(solution)/shard_map/all_gather | solution.py:51
  180.8 2.8 %slice_bitcast_fusion = (bf16[768,768]{0,1:T(8,128)(2,1)S(1)}, bf16[768,768]{1,0:T(8,128)(2,1)}) fusion(bf16[768,1538]{1,0:T(8,128)(2,1)} %all-gather.2.cloned.1.call-done), kind=kLoop, calls=%fused_computation.1 | loop fusion | bytes 4718592 | tf_op jit(solution)/shard_map/transpose | solution.py:54
  183.6 1.4 copy.56
  185.0 1.9 slice_reduce_fusion
  (8 shorter events, 0.1 us)
Async XLA Ops:
  7.2 3.4 %copy-start = (f32[1,768,768]{2,1,0:T(8,128)S(1)}, f32[1,768,768]{2,1,0:T(8,128)}, u32[]{:S(2)}) copy-start(f32[1,768,768]{2,1,0:T(8,128)} %param.13) | copy-start | bytes 7077892
  7.2 98.9 %reduce-scatter.2.cloned.1.call-start = ((), (), s32[]{:S(2)}) async-start(), calls=%async_computation.2 | async-start | bytes 2506752 | tf_op jit(solution)/shard_map/reduce_scatter | solution.py:22
  26.1 0.7 copy-start.5
  26.1 0.7 copy-start.6
  26.1 30.4 %copy-start.7 = (f32[48]{0:T(128)S(1)}, f32[48]{0:T(128)}, u32[]{:S(2)}) copy-start(f32[48]{0:T(128)} %param.19) | copy-start | bytes 580
  26.1 30.4 %copy-start.8 = (f32[48]{0:T(128)S(1)}, f32[48]{0:T(128)}, u32[]{:S(2)}) copy-start(f32[48]{0:T(128)} %param.23) | copy-start | bytes 580
  26.1 30.4 %copy-start.9 = (f32[48]{0:T(128)S(1)}, f32[48]{0:T(128)}, u32[]{:S(2)}) copy-start(f32[48]{0:T(128)} %param.18) | copy-start | bytes 580
  26.1 30.4 %copy-start.10 = (f32[48]{0:T(128)S(1)}, f32[48]{0:T(128)}, u32[]{:S(2)}) copy-start(f32[48]{0:T(128)} %param.22) | copy-start | bytes 580
  26.1 81.2 %copy-start.1 = (f32[48,768]{1,0:T(8,128)S(1)}, f32[48,768]{1,0:T(8,128)}, u32[]{:S(2)}) copy-start(f32[48,768]{1,0:T(8,128)} %param.16) | copy-start | bytes 442372
  26.1 81.2 %copy-start.2 = (f32[48,768]{1,0:T(8,128)S(1)}, f32[48,768]{1,0:T(8,128)}, u32[]{:S(2)}) copy-start(f32[48,768]{1,0:T(8,128)} %param.20) | copy-start | bytes 442372
  26.1 82.0 %copy-start.3 = (f32[768,48]{0,1:T(8,128)S(1)}, f32[768,48]{0,1:T(8,128)}, u32[]{:S(2)}) copy-start(f32[768,48]{0,1:T(8,128)} %param.17) | copy-start | bytes 442372
  26.2 82.0 %copy-start.4 = (f32[768,48]{0,1:T(8,128)S(1)}, f32[768,48]{0,1:T(8,128)}, u32[]{:S(2)}) copy-start(f32[768,48]{0,1:T(8,128)} %param.21) | copy-start | bytes 442372
  27.5 28.9 %all-to-all-start = ((f32[16,1,1536]{2,1,0:T(1,128)}), f32[16,1,1536]{2,1,0:T(1,128)S(1)}, u32[]{:S(2)}, u32[]{:S(2)}) async-start(f32[16,1,1536]{2,1,0:T(1,128)} %broadcast_in_dim.3), calls=%async_computation.1 | async-start | bytes 196608 | tf_op jit(solution)/shard_map/all_to_all | solution.py:32
  42.7 138.0 %all-gather.2.cloned.1.call-start = ((), (), s32[]{:S(2)}) async-start(), calls=%async_computation.3 | async-start | bytes 2715648 | tf_op jit(solution)/shard_map/all_gather | solution.py:51
Sparse Core Ops, SparseCore 0:
  26.3 79.6 reduce-scatter.1
  109.8 70.9 all-gather.1
where the time goes:
time: 194 us
  waiting for transfers between devices  133 us (69%)
  local copies, waits for them, and re-layouts  23.9 us (12%)
  starting transfers between devices  15.3 us (8%)
  between operations  14.2 us (7%)
  other arithmetic  6.85 us (4%)
    all_gather x1, waiting for transfers between devices, gather_turned(): lax.all_gather(both, axis, axis=0, tiled=True)  71.1 us
    reduce_scatter x1, waiting for transfers between devices, one_scatter(): lax.psum_scatter(lines, axis, tiled=True).reshape(-1)  48.7 us
    all_to_all x1, starting transfers between devices, sent_to_all(): return lax.all_to_all(copies, axis, split_axis=0, concat_axis=0, tiled=True)  15.2 us
    all_to_all x1, waiting for transfers between devices, sent_to_all(): return lax.all_to_all(copies, axis, split_axis=0, concat_axis=0, tiled=True)  13.6 us
    reshape x1, local copies, waits for them, and re-layouts, one_scatter(): lines = jnp.concatenate([b.reshape(devices, -1) for b in tiles], axis=1)  7.14 us
  transfers between devices with their start and end apart: 3, of which 3 were waited for; matrix products, arithmetic and copies ran while one was open for 1% of the time, Pallas kernels for 0%

commit v1 on v0

v1 whole, which is shorter than its diff:
```python
import jax
import jax.numpy as jnp
from jax import lax
from jax.sharding import PartitionSpec as P

learn_rate = 0.1
hold_rate = 0.8
up_cuts = [24] * 32
down_cuts = [24] * 30 + [16] * 3


def pieces_of(array, cuts):
    at, pieces = 0, []
    for rows in cuts:
        pieces.append(lax.slice_in_dim(array, at, at + rows))
        at += rows
    return pieces


def on_device(
    partial_up,
    partial_down,
    partial_norm,
    partial_bias,
    master_up,
    master_down,
    master_norm,
    master_bias,
    memory_up,
    memory_down,
    memory_norm,
    memory_bias,
):
    place = lax.axis_index("batch")
    share = master_norm.shape[0]
    mean_rate = lax.axis_size("batch") ** (-0.5)
    kept_rate = learn_rate * hold_rate
    moved_rate = learn_rate * mean_rate

    def kept(master, memory):
        return (master - kept_rate * memory).astype(jnp.bfloat16)

    kept_here = jnp.concatenate([kept(master_up, memory_up), kept(master_down.T, memory_down.T)])
    kept_here, partial_up, partial_down, partial_norm, partial_bias = lax.optimization_barrier(
        (kept_here, partial_up, partial_down, partial_norm, partial_bias)
    )
    kept_all = lax.all_gather(kept_here, "batch")

    def in_place(part):
        whole = jnp.zeros((share * lax.axis_size("batch"),), jnp.bfloat16)
        return lax.dynamic_update_slice_in_dim(whole, part, place * share, 0)

    vectors = jnp.concatenate(
        [
            partial_norm[0].astype(jnp.bfloat16),
            partial_bias[0].astype(jnp.bfloat16),
            in_place(kept(master_norm, memory_norm)),
            in_place(kept(master_bias, memory_bias)),
        ]
    ).reshape(-1, 128)
    ups = pieces_of(partial_up[0].astype(jnp.bfloat16), up_cuts)
    downs = pieces_of(partial_down[0].astype(jnp.bfloat16), down_cuts)
    sums = lax.psum((*ups, *downs, vectors), "batch")
    sum_up = jnp.concatenate(sums[: len(ups)])
    sum_down = jnp.concatenate(sums[len(ups) : -1])
    sum_norm, sum_bias, kept_norm, kept_bias = jnp.split(sums[-1].reshape(-1), 4)
    kept_up = kept_all[:, :share].reshape(sum_up.shape)
    kept_down = kept_all[:, share:].reshape(sum_down.shape).T

    def next_compute(kept, total):
        return (kept.astype(jnp.float32) - moved_rate * total.astype(jnp.float32)).astype(jnp.bfloat16)

    def next_state(master, memory, total, dim):
        here = lax.dynamic_slice_in_dim(total, place * share, share, dim).astype(jnp.float32)
        state = hold_rate * memory + mean_rate * here
        return master - learn_rate * state, state

    stepped_up, state_up = next_state(master_up, memory_up, sum_up, 0)
    stepped_down, state_down = next_state(master_down, memory_down, sum_down, 1)
    stepped_norm, state_norm = next_state(master_norm, memory_norm, sum_norm, 0)
    stepped_bias, state_bias = next_state(master_bias, memory_bias, sum_bias, 0)
    return (
        next_compute(kept_up, sum_up),
        next_compute(kept_down, sum_down),
        next_compute(kept_norm, sum_norm),
        next_compute(kept_bias, sum_bias),
        stepped_up,
        stepped_down,
        stepped_norm,
        stepped_bias,
        state_up,
        state_down,
        state_norm,
        state_bias,
    )


def solution(mesh):
    return jax.shard_map(
        on_device,
        mesh=mesh,
        in_specs=(
            P(("shift", "batch"), None, "cols"),
            P(("shift", "batch"), "cols", None),
            P(("shift", "batch"), None),
            P(("shift", "batch"), None),
            P(("shift", "batch"), "cols"),
            P(("shift", "cols"), "batch"),
            P(("shift", "batch")),
            P(("shift", "batch")),
            P(("shift", "batch"), "cols"),
            P(("shift", "cols"), "batch"),
            P(("shift", "batch")),
            P(("shift", "batch")),
        ),
        out_specs=(
            P("shift", "cols"),
            P(("shift", "cols"), None),
            P("shift"),
            P("shift"),
            P(("shift", "batch"), "cols"),
            P(("shift", "cols"), "batch"),
            P(("shift", "batch")),
            P(("shift", "batch")),
            P(("shift", "batch"), "cols"),
            P(("shift", "cols"), "batch"),
            P(("shift", "batch")),
            P(("shift", "batch")),
        ),
        check_vma=False,
    )
```

time: 194 us -> 167 us (0.86)
  waiting for transfers between devices: 133 us -> 0.02 us
  blocking collectives: 0 us -> 97.2 us
  local copies, waits for them, and re-layouts: 23.9 us -> 39.2 us
  starting transfers between devices: 15.3 us -> 0.04 us
  other arithmetic: 6.85 us -> 14 us
    psum x0 -> x1, blocking collectives: none -> 97.2 us  [on_device(): sums = lax.psum((*ups, *downs, vectors), 'batch')]
    all_gather x1, waiting for transfers between devices: 71.1 us -> 0.01 us  [on_device(): kept_all = lax.all_gather(kept_here, 'batch')]
    reduce_scatter x1 -> x0, waiting for transfers between devices: 48.7 us -> none  [one_scatter(): lax.psum_scatter(lines, axis, tiled=True).reshape(-1)]
    unnamed x24 -> x191, local copies, waits for them, and re-layouts: 3.55 us -> 34.1 us
    all_to_all x1 -> x0, starting transfers between devices: 15.2 us -> none  [sent_to_all(): return lax.all_to_all(copies, axis, split_axis=0, concat_axis=0, tiled=True)]
    all_to_all x1 -> x0, waiting for transfers between devices: 13.6 us -> none  [sent_to_all(): return lax.all_to_all(copies, axis, split_axis=0, concat_axis=0, tiled=True)]
    reshape x4 -> x0, local copies, waits for them, and re-layouts: 9.5 us -> none  [the longest x1 7.14 us: one_scatter(): lines = jnp.concatenate([b.reshape(devices, -1) for b in tiles], axis=1)]
    convert_element_type x2 -> x11, other arithmetic: 2.68 us -> 10.4 us  [the longest x3 4.57 us: next_compute(): (kept.astype(jnp.float32) - moved_rate * total.astype(jnp.float32)).astyp...]
  transfers between devices with their start and end apart: 3 -> 1, of which waited for: 3 -> 0; matrix products, arithmetic and copies ran while one was open for 1% -> 24% of each run, Pallas kernels for 0% -> 0%
where the time goes in v1:
time: 167 us; the launch traced here: 165 us
  blocking collectives  97.2 us (58%)
  local copies, waits for them, and re-layouts  39.2 us (23%)
  between operations  14.8 us (9%)
  other arithmetic  14 us (8%)
    psum x1, blocking collectives, on_device(): sums = lax.psum((*ups, *downs, vectors), 'batch')  97.2 us
    unnamed x191, local copies, waits for them, and re-layouts  34.1 us
    convert_element_type x3, other arithmetic, next_compute(): (kept.astype(jnp.float32) - moved_rate * total.astype(jnp.float32)).astyp...  4.57 us
  transfers between devices with their start and end apart: 1, of which 0 were waited for; matrix products, arithmetic and copies ran while one was open for 24% of the time, Pallas kernels for 0%

profile of v1, /device:TPU:6, one launch (start us, length us, event | category | flops | bytes accessed | tf_op | source)
XLA Modules:
  0.0 165.3 jit_solution(17296802942336737174)
XLA Ops:
  7.2 1.1 subtract_convert_fusion.1
  8.3 1.0 fusion.2
  9.3 0.7 pad_maximum_fusion
  10.4 1.9 %convert_element_type.111 = bf16[1,768,768]{2,1,0:T(8,128)(2,1)S(1)} convert(f32[1,768,768]{2,1,0:T(8,128)} %param.13) | non-fusion elementwise | flops 589824 | bytes 3538944 | tf_op jit(solution)/shard_map/convert_element_type | solution.py:62
  14.1 97.2 %all-reduce.2 = (bf16[24,768]{1,0:T(8,128)(2,1)S(1)}, bf16[24,768]{1,0:T(8,128)(2,1)}, bf16[24,768]{1,0:T(8,128)(2,1)}, bf16[24,768]{1,0:T(8,128)(2,1)}, bf16[24...) all-reduce(bf16[24,768]{1,0:T(8,128)(2,1)S(1)} %get-tuple-element.1, ...), channel_id=1, replica_groups=mesh['shift'=8,'batch'=16,'cols'=4] {'batch'}, use_global_device_ids=true, to_apply=%region_0.0 | all-reduce | flops 1182720 | bytes 4730880 | tf_op jit(solution)/shard_map/psum | solution.py:63
  111.4 0.6 constant_dynamic-update-slice_fusion.31
  112.0 0.8 constant_dynamic-update-slice_fusion.64
  112.8 1.4 constant_dynamic-update-slice_fusion.30
  114.2 0.8 constant_dynamic-update-slice_fusion.63
  115.0 0.8 constant_dynamic-update-slice_fusion.62
  115.7 0.8 constant_dynamic-update-slice_fusion.61
  116.5 0.8 constant_dynamic-update-slice_fusion.60
  117.3 0.8 constant_dynamic-update-slice_fusion.59
  118.1 0.8 constant_dynamic-update-slice_fusion.58
  118.8 0.8 constant_dynamic-update-slice_fusion.57
  119.6 0.8 constant_dynamic-update-slice_fusion.56
  120.4 0.8 constant_dynamic-update-slice_fusion.55
  121.1 0.8 constant_dynamic-update-slice_fusion.54
  121.9 0.8 constant_dynamic-update-slice_fusion.53
  122.7 0.8 constant_dynamic-update-slice_fusion.52
  123.4 0.8 constant_dynamic-update-slice_fusion.51
  125.9 0.8 copy.41
  126.7 0.8 copy.42
  127.5 0.6 constant_dynamic-update-slice_fusion.28
  128.2 0.6 constant_dynamic-update-slice_fusion.27
  128.8 0.6 constant_dynamic-update-slice_fusion.26
  130.0 0.6 constant_dynamic-update-slice_fusion.24
  131.3 0.6 constant_dynamic-update-slice_fusion.22
  131.9 0.6 constant_dynamic-update-slice_fusion.21
  132.5 0.6 constant_dynamic-update-slice_fusion.20
  133.2 0.6 constant_dynamic-update-slice_fusion.19
  134.4 0.6 constant_dynamic-update-slice_fusion.17
  135.6 0.6 constant_dynamic-update-slice_fusion.15
  136.3 0.6 constant_dynamic-update-slice_fusion.14
  137.5 0.6 constant_dynamic-update-slice_fusion.12
  138.8 0.6 constant_dynamic-update-slice_fusion.10
  139.4 0.6 constant_dynamic-update-slice_fusion.9
  140.0 0.6 constant_dynamic-update-slice_fusion.8
  140.6 0.6 constant_dynamic-update-slice_fusion.7
  141.9 0.6 constant_dynamic-update-slice_fusion.5
  143.1 0.6 constant_dynamic-update-slice_fusion.3
  143.7 0.6 constant_dynamic-update-slice_fusion.2
  147.4 1.6 multiply_subtract_fusion.1
  149.0 1.8 %fusion.5 = (bf16[16,48,768]{2,1,0:T(8,128)(2,1)S(1)}, bf16[16,48,768]{2,1,0:T(8,128)(2,1)S(1)}) fusion(bf16[16,96,768]{2,1,0:T(8,128)(2,1)} %bitcast.165), kind=kLoop, calls=%fused_computation.160 | loop fusion | bytes 4718592 | tf_op jit(solution)/shard_map/slice | solution.py:68
  150.8 2.6 %fusion = bf16[768,768]{1,0:T(8,128)(2,1)} fusion(bf16[768,768]{1,0:T(8,128)(2,1)} %constant_dynamic-update-slice_fusion, bf16[16,48,768]{2,1,0:T(8,128)(2,1)S(1)} %get-tuple-element.133), kind=kLoop, calls=%fused_computation.1 | loop fusion | flops 2949120 | bytes 3538944 | tf_op jit(solution)/shard_map/convert_element_type | solution.py:71
  153.4 1.7 %bitcast_convert_fusion = f32[768,768]{1,0:T(8,128)} fusion(bf16[16,48,768]{2,1,0:T(8,128)(2,1)S(1)} %get-tuple-element.132), kind=kLoop, calls=%fused_computation.4 | loop fusion | flops 589824 | bytes 3538944 | tf_op jit(solution)/shard_map/convert_element_type | solution.py:71
  155.1 2.0 %copy.38 = f32[768,768]{0,1:T(8,128)S(1)} copy(f32[768,768]{1,0:T(8,128)} %bitcast_convert_fusion) | data formatting | bytes 4718592 | tf_op jit(solution)/shard_map/convert_element_type | solution.py:71
  157.1 1.3 fusion.1
  (178 shorter events, 11.4 us)
Async XLA Ops:
  7.2 141.8 %all-gather.3.cloned.1.call-start = ((), (), s32[]{:S(2)}) async-start(), calls=%async_computation | async-start | bytes 2506752 | tf_op jit(solution)/shard_map/all_gather | solution.py:47
  111.3 13.0 %copy-start.50 = (bf16[24,768]{1,0:T(8,128)(2,1)S(1)}, bf16[24,768]{1,0:T(8,128)(2,1)}, u32[]{:S(2)}) copy-start(bf16[24,768]{1,0:T(8,128)(2,1)} %get-tuple-element.104) | copy-start | bytes 110596
  111.3 13.0 %copy-start.49 = (bf16[24,768]{1,0:T(8,128)(2,1)S(1)}, bf16[24,768]{1,0:T(8,128)(2,1)}, u32[]{:S(2)}) copy-start(bf16[24,768]{1,0:T(8,128)(2,1)} %get-tuple-element.105) | copy-start | bytes 110596
  111.3 13.0 %copy-start.48 = (bf16[24,768]{1,0:T(8,128)(2,1)S(1)}, bf16[24,768]{1,0:T(8,128)(2,1)}, u32[]{:S(2)}) copy-start(bf16[24,768]{1,0:T(8,128)(2,1)} %get-tuple-element.106) | copy-start | bytes 110596
  111.3 13.0 %copy-start.47 = (bf16[24,768]{1,0:T(8,128)(2,1)S(1)}, bf16[24,768]{1,0:T(8,128)(2,1)}, u32[]{:S(2)}) copy-start(bf16[24,768]{1,0:T(8,128)(2,1)} %get-tuple-element.107) | copy-start | bytes 110596
  111.3 13.0 %copy-start.46 = (bf16[24,768]{1,0:T(8,128)(2,1)S(1)}, bf16[24,768]{1,0:T(8,128)(2,1)}, u32[]{:S(2)}) copy-start(bf16[24,768]{1,0:T(8,128)(2,1)} %get-tuple-element.108) | copy-start | bytes 110596
  111.3 13.0 %copy-start.45 = (bf16[24,768]{1,0:T(8,128)(2,1)S(1)}, bf16[24,768]{1,0:T(8,128)(2,1)}, u32[]{:S(2)}) copy-start(bf16[24,768]{1,0:T(8,128)(2,1)} %get-tuple-element.109) | copy-start | bytes 110596
  111.3 13.1 %copy-start.44 = (bf16[24,768]{1,0:T(8,128)(2,1)S(1)}, bf16[24,768]{1,0:T(8,128)(2,1)}, u32[]{:S(2)}) copy-start(bf16[24,768]{1,0:T(8,128)(2,1)} %get-tuple-element.110) | copy-start | bytes 110596
  111.3 13.1 %copy-start.43 = (bf16[24,768]{1,0:T(8,128)(2,1)S(1)}, bf16[24,768]{1,0:T(8,128)(2,1)}, u32[]{:S(2)}) copy-start(bf16[24,768]{1,0:T(8,128)(2,1)} %get-tuple-element.111) | copy-start | bytes 110596
  111.3 13.1 %copy-start.42 = (bf16[24,768]{1,0:T(8,128)(2,1)S(1)}, bf16[24,768]{1,0:T(8,128)(2,1)}, u32[]{:S(2)}) copy-start(bf16[24,768]{1,0:T(8,128)(2,1)} %get-tuple-element.112) | copy-start | bytes 110596
  111.3 13.1 %copy-start.41 = (bf16[24,768]{1,0:T(8,128)(2,1)S(1)}, bf16[24,768]{1,0:T(8,128)(2,1)}, u32[]{:S(2)}) copy-start(bf16[24,768]{1,0:T(8,128)(2,1)} %get-tuple-element.113) | copy-start | bytes 110596
  111.3 13.1 %copy-start.40 = (bf16[24,768]{1,0:T(8,128)(2,1)S(1)}, bf16[24,768]{1,0:T(8,128)(2,1)}, u32[]{:S(2)}) copy-start(bf16[24,768]{1,0:T(8,128)(2,1)} %get-tuple-element.114) | copy-start | bytes 110596
  111.3 13.1 %copy-start.39 = (bf16[24,768]{1,0:T(8,128)(2,1)S(1)}, bf16[24,768]{1,0:T(8,128)(2,1)}, u32[]{:S(2)}) copy-start(bf16[24,768]{1,0:T(8,128)(2,1)} %get-tuple-element.115) | copy-start | bytes 110596
  111.4 13.1 %copy-start.38 = (bf16[24,768]{1,0:T(8,128)(2,1)S(1)}, bf16[24,768]{1,0:T(8,128)(2,1)}, u32[]{:S(2)}) copy-start(bf16[24,768]{1,0:T(8,128)(2,1)} %get-tuple-element.116) | copy-start | bytes 110596
  111.4 13.2 %copy-start.37 = (bf16[24,768]{1,0:T(8,128)(2,1)S(1)}, bf16[24,768]{1,0:T(8,128)(2,1)}, u32[]{:S(2)}) copy-start(bf16[24,768]{1,0:T(8,128)(2,1)} %get-tuple-element.117) | copy-start | bytes 110596
  111.4 13.2 %copy-start.36 = (bf16[24,768]{1,0:T(8,128)(2,1)S(1)}, bf16[24,768]{1,0:T(8,128)(2,1)}, u32[]{:S(2)}) copy-start(bf16[24,768]{1,0:T(8,128)(2,1)} %get-tuple-element.118) | copy-start | bytes 110596
  111.4 13.2 %copy-start.35 = (bf16[24,768]{1,0:T(8,128)(2,1)S(1)}, bf16[24,768]{1,0:T(8,128)(2,1)}, u32[]{:S(2)}) copy-start(bf16[24,768]{1,0:T(8,128)(2,1)} %get-tuple-element.119) | copy-start | bytes 110596
  112.0 12.6 %copy-start.53 = (bf16[16,768]{1,0:T(8,128)(2,1)S(1)}, bf16[16,768]{1,0:T(8,128)(2,1)}, u32[]{:S(2)}) copy-start(bf16[16,768]{1,0:T(8,128)(2,1)} %get-tuple-element.120) | copy-start | bytes 73732
  112.8 11.8 %copy-start.52 = (bf16[16,768]{1,0:T(8,128)(2,1)S(1)}, bf16[16,768]{1,0:T(8,128)(2,1)}, u32[]{:S(2)}) copy-start(bf16[16,768]{1,0:T(8,128)(2,1)} %get-tuple-element.121) | copy-start | bytes 73732
  112.8 11.8 %copy-start.51 = (bf16[16,768]{1,0:T(8,128)(2,1)S(1)}, bf16[16,768]{1,0:T(8,128)(2,1)}, u32[]{:S(2)}) copy-start(bf16[16,768]{1,0:T(8,128)(2,1)} %get-tuple-element.122) | copy-start | bytes 73732
  124.9 5.8 %copy-start.28 = (bf16[24,768]{1,0:T(8,128)(2,1)S(1)}, bf16[24,768]{1,0:T(8,128)(2,1)}, u32[]{:S(2)}) copy-start(bf16[24,768]{1,0:T(8,128)(2,1)} %get-tuple-element.66) | copy-start | bytes 110596
  124.9 6.4 %copy-start.27 = (bf16[24,768]{1,0:T(8,128)(2,1)S(1)}, bf16[24,768]{1,0:T(8,128)(2,1)}, u32[]{:S(2)}) copy-start(bf16[24,768]{1,0:T(8,128)(2,1)} %get-tuple-element.67) | copy-start | bytes 110596
  124.9 7.0 %copy-start.26 = (bf16[24,768]{1,0:T(8,128)(2,1)S(1)}, bf16[24,768]{1,0:T(8,128)(2,1)}, u32[]{:S(2)}) copy-start(bf16[24,768]{1,0:T(8,128)(2,1)} %get-tuple-element.68) | copy-start | bytes 110596
  124.9 7.6 %copy-start.25 = (bf16[24,768]{1,0:T(8,128)(2,1)S(1)}, bf16[24,768]{1,0:T(8,128)(2,1)}, u32[]{:S(2)}) copy-start(bf16[24,768]{1,0:T(8,128)(2,1)} %get-tuple-element.69) | copy-start | bytes 110596
  124.9 8.2 %copy-start.24 = (bf16[24,768]{1,0:T(8,128)(2,1)S(1)}, bf16[24,768]{1,0:T(8,128)(2,1)}, u32[]{:S(2)}) copy-start(bf16[24,768]{1,0:T(8,128)(2,1)} %get-tuple-element.70) | copy-start | bytes 110596
  124.9 8.8 %copy-start.23 = (bf16[24,768]{1,0:T(8,128)(2,1)S(1)}, bf16[24,768]{1,0:T(8,128)(2,1)}, u32[]{:S(2)}) copy-start(bf16[24,768]{1,0:T(8,128)(2,1)} %get-tuple-element.71) | copy-start | bytes 110596
  124.9 9.5 %copy-start.22 = (bf16[24,768]{1,0:T(8,128)(2,1)S(1)}, bf16[24,768]{1,0:T(8,128)(2,1)}, u32[]{:S(2)}) copy-start(bf16[24,768]{1,0:T(8,128)(2,1)} %get-tuple-element.72) | copy-start | bytes 110596
  124.9 10.1 %copy-start.21 = (bf16[24,768]{1,0:T(8,128)(2,1)S(1)}, bf16[24,768]{1,0:T(8,128)(2,1)}, u32[]{:S(2)}) copy-start(bf16[24,768]{1,0:T(8,128)(2,1)} %get-tuple-element.73) | copy-start | bytes 110596
  125.0 10.7 %copy-start.20 = (bf16[24,768]{1,0:T(8,128)(2,1)S(1)}, bf16[24,768]{1,0:T(8,128)(2,1)}, u32[]{:S(2)}) copy-start(bf16[24,768]{1,0:T(8,128)(2,1)} %get-tuple-element.74) | copy-start | bytes 110596
  125.0 11.3 %copy-start.19 = (bf16[24,768]{1,0:T(8,128)(2,1)S(1)}, bf16[24,768]{1,0:T(8,128)(2,1)}, u32[]{:S(2)}) copy-start(bf16[24,768]{1,0:T(8,128)(2,1)} %get-tuple-element.75) | copy-start | bytes 110596
  125.0 11.9 %copy-start.18 = (bf16[24,768]{1,0:T(8,128)(2,1)S(1)}, bf16[24,768]{1,0:T(8,128)(2,1)}, u32[]{:S(2)}) copy-start(bf16[24,768]{1,0:T(8,128)(2,1)} %get-tuple-element.76) | copy-start | bytes 110596
  125.2 12.3 %copy-start.17 = (bf16[24,768]{1,0:T(8,128)(2,1)S(1)}, bf16[24,768]{1,0:T(8,128)(2,1)}, u32[]{:S(2)}) copy-start(bf16[24,768]{1,0:T(8,128)(2,1)} %get-tuple-element.77) | copy-start | bytes 110596
  125.8 12.3 %copy-start.16 = (bf16[24,768]{1,0:T(8,128)(2,1)S(1)}, bf16[24,768]{1,0:T(8,128)(2,1)}, u32[]{:S(2)}) copy-start(bf16[24,768]{1,0:T(8,128)(2,1)} %get-tuple-element.78) | copy-start | bytes 110596
  125.8 12.9 %copy-start.15 = (bf16[24,768]{1,0:T(8,128)(2,1)S(1)}, bf16[24,768]{1,0:T(8,128)(2,1)}, u32[]{:S(2)}) copy-start(bf16[24,768]{1,0:T(8,128)(2,1)} %get-tuple-element.79) | copy-start | bytes 110596
  125.8 13.5 %copy-start.14 = (bf16[24,768]{1,0:T(8,128)(2,1)S(1)}, bf16[24,768]{1,0:T(8,128)(2,1)}, u32[]{:S(2)}) copy-start(bf16[24,768]{1,0:T(8,128)(2,1)} %get-tuple-element.80) | copy-start | bytes 110596
  125.8 14.2 %copy-start.13 = (bf16[24,768]{1,0:T(8,128)(2,1)S(1)}, bf16[24,768]{1,0:T(8,128)(2,1)}, u32[]{:S(2)}) copy-start(bf16[24,768]{1,0:T(8,128)(2,1)} %get-tuple-element.81) | copy-start | bytes 110596
  126.7 14.0 %copy-start.12 = (bf16[24,768]{1,0:T(8,128)(2,1)S(1)}, bf16[24,768]{1,0:T(8,128)(2,1)}, u32[]{:S(2)}) copy-start(bf16[24,768]{1,0:T(8,128)(2,1)} %get-tuple-element.82) | copy-start | bytes 110596
  126.7 14.6 %copy-start.11 = (bf16[24,768]{1,0:T(8,128)(2,1)S(1)}, bf16[24,768]{1,0:T(8,128)(2,1)}, u32[]{:S(2)}) copy-start(bf16[24,768]{1,0:T(8,128)(2,1)} %get-tuple-element.83) | copy-start | bytes 110596
  126.7 15.2 %copy-start.10 = (bf16[24,768]{1,0:T(8,128)(2,1)S(1)}, bf16[24,768]{1,0:T(8,128)(2,1)}, u32[]{:S(2)}) copy-start(bf16[24,768]{1,0:T(8,128)(2,1)} %get-tuple-element.84) | copy-start | bytes 110596
  126.7 15.8 %copy-start.9 = (bf16[24,768]{1,0:T(8,128)(2,1)S(1)}, bf16[24,768]{1,0:T(8,128)(2,1)}, u32[]{:S(2)}) copy-start(bf16[24,768]{1,0:T(8,128)(2,1)} %get-tuple-element.85) | copy-start | bytes 110596
  126.7 16.4 %copy-start.8 = (bf16[24,768]{1,0:T(8,128)(2,1)S(1)}, bf16[24,768]{1,0:T(8,128)(2,1)}, u32[]{:S(2)}) copy-start(bf16[24,768]{1,0:T(8,128)(2,1)} %get-tuple-element.86) | copy-start | bytes 110596
  126.7 17.1 %copy-start.7 = (bf16[24,768]{1,0:T(8,128)(2,1)S(1)}, bf16[24,768]{1,0:T(8,128)(2,1)}, u32[]{:S(2)}) copy-start(bf16[24,768]{1,0:T(8,128)(2,1)} %get-tuple-element.87) | copy-start | bytes 110596
  126.7 17.7 %copy-start.6 = (bf16[24,768]{1,0:T(8,128)(2,1)S(1)}, bf16[24,768]{1,0:T(8,128)(2,1)}, u32[]{:S(2)}) copy-start(bf16[24,768]{1,0:T(8,128)(2,1)} %get-tuple-element.88) | copy-start | bytes 110596
  127.5 17.5 %copy-start.5 = (bf16[24,768]{1,0:T(8,128)(2,1)S(1)}, bf16[24,768]{1,0:T(8,128)(2,1)}, u32[]{:S(2)}) copy-start(bf16[24,768]{1,0:T(8,128)(2,1)} %get-tuple-element.89) | copy-start | bytes 110596
  127.5 18.7 %copy-start.59 = (f32[48]{0:T(128)S(1)}, f32[48]{0:T(128)}, u32[]{:S(2)}) copy-start(f32[48]{0:T(128)} %param.18) | copy-start | bytes 580
  127.5 18.7 %copy-start.61 = (f32[48]{0:T(128)S(1)}, f32[48]{0:T(128)}, u32[]{:S(2)}) copy-start(f32[48]{0:T(128)} %param.22) | copy-start | bytes 580
  127.5 19.9 %copy-start.3 = (f32[48,768]{1,0:T(8,128)S(1)}, f32[48,768]{1,0:T(8,128)}, u32[]{:S(2)}) copy-start(f32[48,768]{1,0:T(8,128)} %param.16) | copy-start | bytes 442372
  127.5 19.9 %copy-start.4 = (f32[48,768]{1,0:T(8,128)S(1)}, f32[48,768]{1,0:T(8,128)}, u32[]{:S(2)}) copy-start(f32[48,768]{1,0:T(8,128)} %param.20) | copy-start | bytes 442372
  (15 other events, 34.4 us)
Sparse Core Ops, SparseCore 0:
  10.7 83.4 all-gather.2
